TPU v7x, 32 devices: a whole 2x2x4 slice. The times are simulated.
32 devices in a mesh: grp: 8 (over y, x, core), mem: 4 (over z).
Axes of the slice: x: 2, y: 2, z: 4, core: 2. Of those that a mesh axis runs over, the one named last changes fastest.
Arguments:
- residual: float32 [256, 64, 256], P(('grp', 'mem')), may hold values from -6 to 6
- direction: float32 [256, 64, 256], P(('grp', 'mem')), may hold values from -6 to 6
- local_inverse: bfloat16 [256, 256, 256], P(('grp', 'mem')), may hold values from -1 to 16, as said below
- dirichlet: bfloat16 [256, 256, 256], P(('grp', 'mem')), may hold values from -1 to 16, as said below
- coupling: bfloat16 [256, 24, 256], P(('grp', 'mem')), may hold values from -0.375 to 0.375
- corner_map: int32 [256, 24], P(('grp', 'mem')), may hold values from 0 to 6143
- coarse_factor: bfloat16 [8, 2048, 2048], P('grp'), may hold values from -1 to 3, as said below
Outputs:
- new_residual: float32 [256, 64, 256], P(('grp', 'mem'))
- new_direction: float32 [256, 64, 256], P(('grp', 'mem'))
- step_sizes: float32 [3, 64], replicated
Inputs may be any that keep to these rules, and one draw needn't show every extreme that they name: `local_inverse`: each subdomain's matrix is symmetric positive definite. `dirichlet`: each subdomain's matrix is symmetric positive definite. `coarse_factor`: each group's factor is lower triangular with a positive diagonal.
All inputs are finite; a program needn't handle non-finite values.
Results may differ from a plain program's by a relative error of at most 0.0083.
Values sent between devices are 32-bit elements; how exact they have to be, the bound alone decides.
A program may use at most 128 MiB of HBM per device.

v0:
```python
import jax
import jax.numpy as jnp
from jax import lax
from jax.sharding import PartitionSpec as P

ITERS = 3
highest = lax.Precision.HIGHEST


def from_behind(block, axis, distance):
    devices = range(lax.axis_size(axis))
    route = [((i - distance) % len(devices), i) for i in devices]
    return lax.ppermute(block, axis, route)


def extended(cells, sides, width):
    for axis, dim in sides:
        count = lax.axis_size(axis)
        head = lax.slice_in_dim(cells, 0, width, axis=dim)
        tail = lax.slice_in_dim(cells, cells.shape[dim] - width, cells.shape[dim], axis=dim)
        cells = jnp.concatenate(
            [
                lax.ppermute(tail, axis, [(i, (i + 1) % count) for i in range(count)]),
                cells,
                lax.ppermute(head, axis, [((i + 1) % count, i) for i in range(count)]),
            ],
            axis=dim,
        )
    return cells


def solve_local(matrices, vectors):
    return jnp.einsum(
        "sij,skj->ski", matrices, vectors.astype(jnp.bfloat16), preferred_element_type=jnp.float32
    )


def column_sums(left_side, right_side):
    return jnp.sum(left_side * right_side, axis=(0, 2))


def coarse_solve(factor, coarse_load):
    forward = jax.scipy.linalg.solve_triangular(factor, coarse_load.T, lower=True)
    return jax.scipy.linalg.solve_triangular(factor, forward, lower=True, trans=1).T


def fold_neighbours(partial_value, block_size):
    from_upper = from_behind(partial_value[:, :block_size], "grp", -1)
    from_lower = from_behind(partial_value[:, 2 * block_size :], "grp", 1)
    return partial_value[:, block_size : 2 * block_size] + from_upper + from_lower


def local(residual, direction, local_inverse, dirichlet, coupling, corner_map, coarse_factor):
    sub_count, rhs_count, dofs_count = residual.shape
    corner_count = coupling.shape[1]
    block_size = coarse_factor.shape[1]
    factor = coarse_factor[0].astype(jnp.float32)
    flat_map = corner_map.reshape(-1)
    coupling_wide = coupling.astype(jnp.float32)
    precond = solve_local(dirichlet, residual)
    norm_now = lax.psum(column_sums(residual, precond), ("grp", "mem"))
    step_list = []
    for iteration in range(ITERS):
        solved = solve_local(local_inverse, direction)
        partial_corner = jnp.einsum("ski,sci->skc", solved, coupling_wide, precision=highest)
        flat_corner = partial_corner.transpose(1, 0, 2).reshape(rhs_count, sub_count * corner_count)
        partial_value = (
            jnp.zeros((rhs_count, 3 * block_size), jnp.float32).at[:, flat_map].add(flat_corner)
        )
        folded = fold_neighbours(partial_value, block_size)
        solution = coarse_solve(factor, lax.psum(folded, "mem"))
        widened = extended(solution, (("grp", 1),), block_size)
        picked = widened[:, flat_map].reshape(rhs_count, sub_count, corner_count).transpose(1, 0, 2)
        lifted = jnp.einsum("skc,sci->ski", picked, coupling_wide, precision=highest)
        image = solve_local(local_inverse, direction + lifted)
        curvature = lax.psum(column_sums(direction, image), ("grp", "mem"))
        alpha = norm_now / curvature
        step_list.append(alpha)
        residual = residual - alpha[None, :, None] * image
        precond = solve_local(dirichlet, residual)
        norm_next = lax.psum(column_sums(residual, precond), ("grp", "mem"))
        direction = precond + (norm_next / norm_now)[None, :, None] * direction
        norm_now = norm_next
    return (residual, direction, jnp.stack(step_list))


def solution(mesh):
    return jax.shard_map(
        local,
        mesh=mesh,
        in_specs=(
            P(("grp", "mem"), None, None),
            P(("grp", "mem"), None, None),
            P(("grp", "mem"), None, None),
            P(("grp", "mem"), None, None),
            P(("grp", "mem"), None, None),
            P(("grp", "mem"), None),
            P("grp", None, None),
        ),
        out_specs=(P(("grp", "mem"), None, None), P(("grp", "mem"), None, None), P()),
        check_vma=False,
    )
```

profile of v0, /device:TPU:0, one launch (start us, length us, event | category | flops | bytes accessed | tf_op | source)
XLA Modules:
  0.0 917.9 jit_solution(7679273841835778049)
XLA Ops:
  11.1 3.0 scatter_custom_fusion
  14.1 3.0 fusion.365
  24.0 11.3 %convert_select_fusion = f32[2048,2048]{1,0:T(8,128)} fusion(bf16[1,2048,2048]{2,1,0:T(8,128)(2,1)} %param.17), kind=kLoop, calls=%fused_computation.8 | loop fusion | flops 12582912 | bytes 25165824 | tf_op jit(solution)/shard_map/jit(_solve_triangular)/triangular_solve | solution.py:44
  37.6 55.7 %while.12 = (s32[]{:T(128)}, f32[2048,2048]{1,0:T(8,128)}, s32[16,2]{0,1:T(2,128)S(1)}, f32[16,128,128]{2,1,0:T(8,128)}, s32[]{:T(128)}) while((s32[]{:T(128)}, f32[2048,2048]{1,0:T(8,128)}, s32[16,2]{0,1:T(2,128)S(1)}, f32[16,128,128]{2,1,0:T(8,128)}, s32[]{:T(128)}) %tuple.417), condition=%wide.while_cond.1, body=%wide.while_body.1.sunk | while | flops 2 | bytes 132205 | solution.py:44
  38.2 2.9 bitcast_dynamic-update-slice_fusion.2
  45.2 2.9 bitcast_dynamic-update-slice_fusion.2
  55.7 2.9 bitcast_dynamic-update-slice_fusion.2
  59.2 2.9 bitcast_dynamic-update-slice_fusion.2
  62.6 2.9 bitcast_dynamic-update-slice_fusion.2
  73.1 2.9 bitcast_dynamic-update-slice_fusion.2
  83.6 2.9 bitcast_dynamic-update-slice_fusion.2
  93.3 158.4 %custom-call.11 = f32[16,128,128]{1,2,0:T(8,128)S(1)} custom-call(f32[16,128,128]{2,1,0:T(8,128)} %get-tuple-element.46), custom_call_target="InvertDiagBlocksLowerTriangular" | custom-call | tf_op jit(solution)/shard_map/jit(_solve_triangular)/triangular_solve | solution.py:44
  308.3 11.7 %collective-permute-done.3 = f32[64,2048]{1,0:T(8,128)S(1)} collective-permute-done((f32[64,2048]{1,0:T(8,128)S(1)}, f32[64,2048]{1,0:T(8,128)S(1)}, u32[]{:S(2)}, u32[]{:S(2)}) %collective-permute-start.3) | collective-permute-done | bytes 524320 | tf_op jit(solution)/shard_map/ppermute | solution.py:25
  322.5 3.2 copy.31
  332.1 39.5 %all-reduce = (f32[64]{0:T(128)S(1)}, f32[64]{0:T(128)S(1)}) all-reduce(f32[64]{0:T(128)S(1)} %fusion.9, f32[64]{0:T(128)S(1)} %get-tuple-element.437), channel_id=1, replica_groups=mesh['grp'=8,'mem'=4] {'grp','mem'}, use_global_device_ids=true, to_apply=%region_1.0 | all-reduce | flops 128 | bytes 1024 | tf_op jit(solution)/shard_map/psum | solution.py:61
  375.1 40.9 %psum.73 = f32[64]{0:T(128)S(1)} all-reduce(f32[64]{0:T(128)S(1)} %get-tuple-element.439), channel_id=1, replica_groups=mesh['grp'=8,'mem'=4] {'grp','mem'}, use_global_device_ids=true, to_apply=%region_7.0 | all-reduce | flops 64 | bytes 512 | tf_op jit(solution)/shard_map/psum | solution.py:81
  419.0 3.0 scatter_custom_fusion.1
  422.0 3.6 fusion.364
  435.3 8.7 collective-permute-done.5
  447.3 38.6 %all-reduce.7.cloned.1.call-done = f32[2048,64]{0,1:T(8,128)} async-done(((f32[2048,64]{0,1:T(8,128)}), f32[2048,64]{0,1:T(8,128)}) %all-reduce.7.cloned.1.call-update) | async-done | bytes 524304 | tf_op jit(solution)/shard_map/psum | solution.py:71
  556.5 12.2 %collective-permute-done.7 = f32[64,2048]{1,0:T(8,128)S(1)} collective-permute-done((f32[64,2048]{1,0:T(8,128)S(1)}, f32[64,2048]{1,0:T(8,128)S(1)}, u32[]{:S(2)}, u32[]{:S(2)}) %collective-permute-start.7) | collective-permute-done | bytes 524320 | tf_op jit(solution)/shard_map/ppermute | solution.py:25
  572.0 3.2 copy.35
  581.7 39.3 %psum.75 = f32[64]{0:T(128)S(1)} all-reduce(f32[64]{0:T(128)S(1)} %get-tuple-element.479), channel_id=1, replica_groups=mesh['grp'=8,'mem'=4] {'grp','mem'}, use_global_device_ids=true, to_apply=%region_11.0 | all-reduce | flops 64 | bytes 512 | tf_op jit(solution)/shard_map/psum | solution.py:76
  624.5 38.9 %psum.76 = f32[64]{0:T(128)S(1)} all-reduce(f32[64]{0:T(128)S(1)} %get-tuple-element.481), channel_id=1, replica_groups=mesh['grp'=8,'mem'=4] {'grp','mem'}, use_global_device_ids=true, to_apply=%region_13.0 | all-reduce | flops 64 | bytes 512 | tf_op jit(solution)/shard_map/psum | solution.py:81
  666.4 3.0 scatter_custom_fusion.2
  669.4 3.6 fusion.363
  682.9 7.5 collective-permute-done.9
  694.3 39.1 %all-reduce.9.cloned.1.call-done = f32[2048,64]{0,1:T(8,128)} async-done(((f32[2048,64]{0,1:T(8,128)}), f32[2048,64]{0,1:T(8,128)}) %all-reduce.9.cloned.1.call-update) | async-done | bytes 524304 | tf_op jit(solution)/shard_map/psum | solution.py:71
  804.0 12.3 %collective-permute-done.11 = f32[64,2048]{1,0:T(8,128)S(1)} collective-permute-done((f32[64,2048]{1,0:T(8,128)S(1)}, f32[64,2048]{1,0:T(8,128)S(1)}, u32[]{:S(2)}, u32[]{:S(2)}) %collective-permute-start.11) | collective-permute-done | bytes 524320 | tf_op jit(solution)/shard_map/ppermute | solution.py:25
  819.5 3.2 copy.39
  828.4 39.3 %psum.78 = f32[64]{0:T(128)S(1)} all-reduce(f32[64]{0:T(128)S(1)} %get-tuple-element.521), channel_id=1, replica_groups=mesh['grp'=8,'mem'=4] {'grp','mem'}, use_global_device_ids=true, to_apply=%region_17.0 | all-reduce | flops 64 | bytes 512 | tf_op jit(solution)/shard_map/psum | solution.py:76
  869.4 38.9 %psum.79 = f32[64]{0:T(128)S(1)} all-reduce(f32[64]{0:T(128)S(1)} %get-tuple-element.523), channel_id=1, replica_groups=mesh['grp'=8,'mem'=4] {'grp','mem'}, use_global_device_ids=true, to_apply=%region_19.0 | all-reduce | flops 64 | bytes 512 | tf_op jit(solution)/shard_map/psum | solution.py:81
  (668 shorter events, 313.8 us)
Async XLA Ops:
  7.2 1.2 copy-start
  7.2 244.6 %all-reduce.5.cloned.1.call-start = ((), (), s32[]{:S(2)}) async-start(), calls=%async_computation | async-start | bytes 1048576 | tf_op jit(solution)/shard_map/psum | solution.py:71
  19.5 16.1 %collective-permute-start.1 = (f32[64,2048]{1,0:T(8,128)}, f32[64,2048]{1,0:T(8,128)}, u32[]{:S(2)}, u32[]{:S(2)}) collective-permute-start(f32[64,2048]{1,0:T(8,128)} %copy.30), channel_id=1, source_target_pairs={{28,0},{0,4},{4,8},{8,12},{12,16},{16,20},{20,24},{24,28},{29,1},{... | collective-permute-start | bytes 1572872 | tf_op jit(solution)/shard_map/ppermute | solution.py:13
  21.1 14.5 %collective-permute-start = (f32[64,2048]{1,0:T(8,128)}, f32[64,2048]{1,0:T(8,128)S(1)}, u32[]{:S(2)}, u32[]{:S(2)}) collective-permute-start(f32[64,2048]{1,0:T(8,128)} %copy.29), channel_id=1, source_target_pairs={{4,0},{8,4},{12,8},{16,12},{20,16},{24,20},{28,24},{0,28},{5,1},{9... | collective-permute-start | bytes 1572872 | tf_op jit(solution)/shard_map/ppermute | solution.py:13
  37.6 448.3 %all-reduce.7.cloned.1.call-start = ((), (), s32[]{:S(2)}) async-start(), calls=%async_computation.1 | async-start | bytes 1048576 | tf_op jit(solution)/shard_map/psum | solution.py:71
  251.8 39.4 %copy-start.1 = (f32[2048,2048]{1,0:T(8,128)S(1)}, f32[2048,2048]{1,0:T(8,128)}, u32[]{:S(2)}) copy-start(f32[2048,2048]{1,0:T(8,128)} %get-tuple-element.572) | copy-start | bytes 50331652
  272.1 35.6 %copy-start.2 = (bf16[8,256,256]{2,1,0:T(8,128)(2,1)S(1)}, bf16[8,256,256]{2,1,0:T(8,128)(2,1)}, u32[]{:S(2)}) copy-start(bf16[8,256,256]{2,1,0:T(8,128)(2,1)} %param.14) | copy-start | bytes 3145732
  272.1 35.6 %copy-start.9 = (f32[8,64,256]{2,1,0:T(8,128)S(1)}, f32[8,64,256]{2,1,0:T(8,128)}, u32[]{:S(2)}) copy-start(f32[8,64,256]{2,1,0:T(8,128)} %param.11) | copy-start | bytes 1572868
  292.3 35.9 %copy-start.7 = (bf16[8,24,256]{2,1,0:T(8,128)(2,1)S(1)}, bf16[8,24,256]{2,1,0:T(8,128)(2,1)}, u32[]{:S(2)}) copy-start(bf16[8,24,256]{2,1,0:T(8,128)(2,1)} %param.15) | copy-start | bytes 294916
  306.0 13.9 %collective-permute-start.3 = (f32[64,2048]{1,0:T(8,128)S(1)}, f32[64,2048]{1,0:T(8,128)S(1)}, u32[]{:S(2)}, u32[]{:S(2)}) collective-permute-start(f32[64,2048]{1,0:T(8,128)S(1)} %bitcast.583), channel_id=1, source_target_pairs={{4,0},{8,4},{12,8},{16,12},{20,16},{24,20},{28,24},{0,28},{5,1},{9... | collective-permute-start | bytes 1572872 | tf_op jit(solution)/shard_map/ppermute | solution.py:25
  307.7 13.5 %collective-permute-start.2 = (f32[64,2048]{1,0:T(8,128)S(1)}, f32[64,2048]{1,0:T(8,128)S(1)}, u32[]{:S(2)}, u32[]{:S(2)}) collective-permute-start(f32[64,2048]{1,0:T(8,128)S(1)} %bitcast.584), channel_id=1, source_target_pairs={{0,4},{4,8},{8,12},{12,16},{16,20},{20,24},{24,28},{28,0},{1,5},{5... | collective-permute-start | bytes 1572872 | tf_op jit(solution)/shard_map/ppermute | solution.py:23
  373.0 0.8 copy-start.6
  417.4 0.8 copy-start.4
  430.3 13.7 %collective-permute-start.5 = (f32[64,2048]{1,0:T(8,128)}, f32[64,2048]{1,0:T(8,128)}, u32[]{:S(2)}, u32[]{:S(2)}) collective-permute-start(f32[64,2048]{1,0:T(8,128)} %copy.34), channel_id=1, source_target_pairs={{28,0},{0,4},{4,8},{8,12},{12,16},{16,20},{20,24},{24,28},{29,1},{... | collective-permute-start | bytes 1572872 | tf_op jit(solution)/shard_map/ppermute | solution.py:13
  430.3 14.3 %collective-permute-start.4 = (f32[64,2048]{1,0:T(8,128)}, f32[64,2048]{1,0:T(8,128)}, u32[]{:S(2)}, u32[]{:S(2)}) collective-permute-start(f32[64,2048]{1,0:T(8,128)} %copy.33), channel_id=1, source_target_pairs={{4,0},{8,4},{12,8},{16,12},{20,16},{24,20},{28,24},{0,28},{5,1},{9... | collective-permute-start | bytes 1572872 | tf_op jit(solution)/shard_map/ppermute | solution.py:13
  446.9 286.5 %all-reduce.9.cloned.1.call-start = ((), (), s32[]{:S(2)}) async-start(), calls=%async_computation.2 | async-start | bytes 1048576 | tf_op jit(solution)/shard_map/psum | solution.py:71
  555.6 13.2 %collective-permute-start.7 = (f32[64,2048]{1,0:T(8,128)S(1)}, f32[64,2048]{1,0:T(8,128)S(1)}, u32[]{:S(2)}, u32[]{:S(2)}) collective-permute-start(f32[64,2048]{1,0:T(8,128)S(1)} %bitcast.586), channel_id=1, source_target_pairs={{4,0},{8,4},{12,8},{16,12},{20,16},{24,20},{28,24},{0,28},{5,1},{9... | collective-permute-start | bytes 1572872 | tf_op jit(solution)/shard_map/ppermute | solution.py:25
  556.5 14.3 %collective-permute-start.6 = (f32[64,2048]{1,0:T(8,128)S(1)}, f32[64,2048]{1,0:T(8,128)S(1)}, u32[]{:S(2)}, u32[]{:S(2)}) collective-permute-start(f32[64,2048]{1,0:T(8,128)S(1)} %bitcast.587), channel_id=1, source_target_pairs={{0,4},{4,8},{8,12},{12,16},{16,20},{20,24},{24,28},{28,0},{1,5},{5... | collective-permute-start | bytes 1572872 | tf_op jit(solution)/shard_map/ppermute | solution.py:23
  622.4 0.8 copy-start.5
  664.8 0.8 copy-start.3
  677.7 12.7 %collective-permute-start.9 = (f32[64,2048]{1,0:T(8,128)}, f32[64,2048]{1,0:T(8,128)}, u32[]{:S(2)}, u32[]{:S(2)}) collective-permute-start(f32[64,2048]{1,0:T(8,128)} %copy.38), channel_id=1, source_target_pairs={{28,0},{0,4},{4,8},{8,12},{12,16},{16,20},{20,24},{24,28},{29,1},{... | collective-permute-start | bytes 1572872 | tf_op jit(solution)/shard_map/ppermute | solution.py:13
  677.7 14.3 %collective-permute-start.8 = (f32[64,2048]{1,0:T(8,128)}, f32[64,2048]{1,0:T(8,128)}, u32[]{:S(2)}, u32[]{:S(2)}) collective-permute-start(f32[64,2048]{1,0:T(8,128)} %copy.37), channel_id=1, source_target_pairs={{4,0},{8,4},{12,8},{16,12},{20,16},{24,20},{28,24},{0,28},{5,1},{9... | collective-permute-start | bytes 1572872 | tf_op jit(solution)/shard_map/ppermute | solution.py:13
  803.1 13.2 %collective-permute-start.11 = (f32[64,2048]{1,0:T(8,128)S(1)}, f32[64,2048]{1,0:T(8,128)S(1)}, u32[]{:S(2)}, u32[]{:S(2)}) collective-permute-start(f32[64,2048]{1,0:T(8,128)S(1)} %bitcast.580), channel_id=1, source_target_pairs={{4,0},{8,4},{12,8},{16,12},{20,16},{24,20},{28,24},{0,28},{5,1},{9... | collective-permute-start | bytes 1572872 | tf_op jit(solution)/shard_map/ppermute | solution.py:25
  804.0 14.3 %collective-permute-start.10 = (f32[64,2048]{1,0:T(8,128)S(1)}, f32[64,2048]{1,0:T(8,128)S(1)}, u32[]{:S(2)}, u32[]{:S(2)}) collective-permute-start(f32[64,2048]{1,0:T(8,128)S(1)} %bitcast.581), channel_id=1, source_target_pairs={{0,4},{4,8},{8,12},{12,16},{16,20},{20,24},{24,28},{28,0},{1,5},{5... | collective-permute-start | bytes 1572872 | tf_op jit(solution)/shard_map/ppermute | solution.py:23
  868.9 42.0 %copy-start.8 = (f32[8,64,256]{2,1,0:T(8,128)}, f32[8,64,256]{2,1,0:T(8,128)S(1)}, u32[]{:S(2)}) copy-start(f32[8,64,256]{2,1,0:T(8,128)S(1)} %multiply_subtract_fusion) | copy-start | bytes 1572868
Sparse Core Ops, SparseCore 0:
  37.7 39.7 all-reduce.4
  447.0 38.8 all-reduce.6
  694.4 38.9 all-reduce.8
where the time goes:
time: 931 us; the launch traced here: 918 us
  blocking collectives  237 us (25%)
  matrix products  207 us (22%)
  other arithmetic  198 us (21%)
  waiting for transfers between devices  138 us (15%)
  local copies, waits for them, and re-layouts  107 us (11%)
  between operations  18.2 us (2%)
  starting transfers between devices  12.9 us (1%)
    another operation x4, other arithmetic, coarse_solve(): jax.scipy.linalg.solve_triangular(factor, forward, lower=True, trans=1)  170 us
    another operation x93, matrix products, coarse_solve(): jax.scipy.linalg.solve_triangular(factor, coarse_load.T, lower=True)  124 us
    psum x3, blocking collectives, local(): norm_next = lax.psum(column_sums(residual, precond), ('grp', 'mem'))  119 us
    psum x2, blocking collectives, local(): curvature = lax.psum(column_sums(direction, image), ('grp', 'mem'))  78.5 us
    psum x3, waiting for transfers between devices, local(): solution = coarse_solve(factor, lax.psum(folded, 'mem'))  77.7 us
    another operation x93, matrix products, coarse_solve(): jax.scipy.linalg.solve_triangular(factor, forward, lower=True, trans=1)  64.3 us
    another operation x85, local copies, waits for them, and re-layouts, coarse_solve(): jax.scipy.linalg.solve_triangular(factor, forward, lower=True, trans=1)  55.9 us
    psum x1, blocking collectives, local(): norm_now = lax.psum(column_sums(residual, precond), ('grp', 'mem'))  39.5 us
  transfers between devices with their start and end apart: 15, of which 12 were waited for; matrix products, arithmetic and copies ran while one was open for 25% of the time, Pallas kernels for 0%

commit v1 on v0

--- a/solution.py
+++ b/solution.py
@@ -73,7 +73,8 @@
         picked = widened[:, flat_map].reshape(rhs_count, sub_count, corner_count).transpose(1, 0, 2)
         lifted = jnp.einsum("skc,sci->ski", picked, coupling_wide, precision=highest)
         image = solve_local(local_inverse, direction + lifted)
-        curvature = lax.psum(column_sums(direction, image), ("grp", "mem"))
+        arr_in = column_sums(direction, image)
+        curvature = jax.lax.all_gather(arr_in, ("grp", "mem")).sum(axis=0)
         alpha = norm_now / curvature
         step_list.append(alpha)
         residual = residual - alpha[None, :, None] * image

time: 931 us -> 938 us (level)
  local copies, waits for them, and re-layouts: 107 us -> 118 us
  waiting for transfers between devices: 138 us -> 127 us
    unnamed x0 -> x2, blocking collectives: none -> 80.7 us
    psum x2 -> x0, blocking collectives: 78.5 us -> none  [local(): curvature = lax.psum(column_sums(direction, image), ('grp', 'mem'))]
    ppermute x3, waiting for transfers between devices: 36.2 us -> 0.01 us  [extended(): lax.ppermute(head, axis, [((i + 1) % count, i) for i in range(count)])]
    ppermute x3, waiting for transfers between devices: 5.2 us -> 31.6 us  [extended(): lax.ppermute(tail, axis, [(i, (i + 1) % count) for i in range(count)])]
    unnamed x329 -> x333, local copies, waits for them, and re-layouts: 10.1 us -> 19.5 us
  transfers between devices with their start and end apart: 15 -> 15, of which waited for: 12 -> 10; matrix products, arithmetic and copies ran while one was open for 25% -> 26% of each run, Pallas kernels for 0% -> 0%
where the time goes in v1:
time: 938 us; the launch traced here: 925 us
  blocking collectives  240 us (26%)
  matrix products  209 us (22%)
  other arithmetic  199 us (21%)
  waiting for transfers between devices  127 us (14%)
  local copies, waits for them, and re-layouts  118 us (13%)
  between operations  17.9 us (2%)
  starting transfers between devices  13.7 us (1%)
    another operation x4, other arithmetic, coarse_solve(): jax.scipy.linalg.solve_triangular(factor, forward, lower=True, trans=1)  169 us
    another operation x93, matrix products, coarse_solve(): jax.scipy.linalg.solve_triangular(factor, coarse_load.T, lower=True)  124 us
    psum x3, blocking collectives, local(): norm_next = lax.psum(column_sums(residual, precond), ('grp', 'mem'))  120 us
    unnamed x2, blocking collectives  80.7 us
    psum x3, waiting for transfers between devices, local(): solution = coarse_solve(factor, lax.psum(folded, 'mem'))  74 us
    another operation x93, matrix products, coarse_solve(): jax.scipy.linalg.solve_triangular(factor, forward, lower=True, trans=1)  65.3 us
    another operation x85, local copies, waits for them, and re-layouts, coarse_solve(): jax.scipy.linalg.solve_triangular(factor, forward, lower=True, trans=1)  57.2 us
    psum x1, blocking collectives, local(): norm_now = lax.psum(column_sums(residual, precond), ('grp', 'mem'))  39.6 us
  transfers between devices with their start and end apart: 15, of which 10 were waited for; matrix products, arithmetic and copies ran while one was open for 26% of the time, Pallas kernels for 0%

profile of v1, /device:TPU:0, one launch (start us, length us, event | category | flops | bytes accessed | tf_op | source)
XLA Modules:
  0.0 924.7 jit_solution(10026663433563119367)
XLA Ops:
  11.1 3.0 scatter_custom_fusion
  14.2 3.0 fusion.365
  19.5 3.4 collective-permute-start
  24.0 11.3 %convert_select_fusion = f32[2048,2048]{1,0:T(8,128)} fusion(bf16[1,2048,2048]{2,1,0:T(8,128)(2,1)} %param.17), kind=kLoop, calls=%fused_computation.8 | loop fusion | flops 12582912 | bytes 25165824 | tf_op jit(solution)/shard_map/jit(_solve_triangular)/triangular_solve | solution.py:44
  38.4 56.4 %while.12 = (s32[]{:T(128)}, f32[2048,2048]{1,0:T(8,128)}, s32[16,2]{0,1:T(2,128)S(1)}, f32[16,128,128]{2,1,0:T(8,128)}, s32[]{:T(128)}) while((s32[]{:T(128)}, f32[2048,2048]{1,0:T(8,128)}, s32[16,2]{0,1:T(2,128)S(1)}, f32[16,128,128]{2,1,0:T(8,128)}, s32[]{:T(128)}) %tuple.417), condition=%wide.while_cond.1, body=%wide.while_body.1.sunk | while | flops 2 | bytes 132705 | solution.py:44
  42.6 2.9 bitcast_dynamic-update-slice_fusion.2
  56.7 2.9 bitcast_dynamic-update-slice_fusion.2
  63.8 2.9 bitcast_dynamic-update-slice_fusion.2
  67.3 2.9 bitcast_dynamic-update-slice_fusion.2
  94.8 158.1 %custom-call.11 = f32[16,128,128]{1,2,0:T(8,128)S(1)} custom-call(f32[16,128,128]{2,1,0:T(8,128)} %get-tuple-element.46), custom_call_target="InvertDiagBlocksLowerTriangular" | custom-call | tf_op jit(solution)/shard_map/jit(_solve_triangular)/triangular_solve | solution.py:44
  321.5 10.2 %collective-permute-done.2 = f32[64,2048]{1,0:T(8,128)} collective-permute-done((f32[64,2048]{1,0:T(8,128)}, f32[64,2048]{1,0:T(8,128)}, u32[]{:S(2)}, u32[]{:S(2)}) %collective-permute-start.2) | collective-permute-done | bytes 524320 | tf_op jit(solution)/shard_map/ppermute | solution.py:23
  334.4 3.2 copy.31
  344.3 39.6 %all-reduce.3 = (f32[64]{0:T(128)S(1)}, f32[2048]{0:T(1024)S(1)}) all-reduce(f32[64]{0:T(128)S(1)} %fusion.9, f32[2048]{0:T(1024)S(1)} %dynamic-update-slice.8), channel_id=1, replica_groups=mesh['grp'=8,'mem'=4] {'grp','mem'}, use_global_device_ids=true, to_apply=%region_1.0 | all-reduce | flops 2112 | bytes 16896 | tf_op jit(solution)/shard_map/psum | solution.py:61
  387.5 40.2 %psum.51 = f32[64]{0:T(128)S(1)} all-reduce(f32[64]{0:T(128)S(1)} %get-tuple-element.439), channel_id=1, replica_groups=mesh['grp'=8,'mem'=4] {'grp','mem'}, use_global_device_ids=true, to_apply=%region_7.0 | all-reduce | flops 64 | bytes 512 | tf_op jit(solution)/shard_map/psum | solution.py:82
  430.7 3.0 scatter_custom_fusion.1
  433.7 3.6 fusion.364
  445.2 4.8 collective-permute-done.4
  450.0 5.8 collective-permute-done.5
  458.3 36.6 %all-reduce.10.cloned.1.call-done = f32[2048,64]{0,1:T(8,128)} async-done(((f32[2048,64]{0,1:T(8,128)}), f32[2048,64]{0,1:T(8,128)}) %all-reduce.10.cloned.1.call-update) | async-done | bytes 524304 | tf_op jit(solution)/shard_map/psum | solution.py:71
  567.5 10.7 %collective-permute-done.6 = f32[64,2048]{1,0:T(8,128)S(1)} collective-permute-done((f32[64,2048]{1,0:T(8,128)S(1)}, f32[64,2048]{1,0:T(8,128)S(1)}, u32[]{:S(2)}, u32[]{:S(2)}) %collective-permute-start.6) | collective-permute-done | bytes 524320 | tf_op jit(solution)/shard_map/ppermute | solution.py:23
  579.4 3.2 copy.35
  589.4 40.3 %all-reduce.1 = f32[2048]{0:T(1024)S(1)} all-reduce(f32[2048]{0:T(1024)S(1)} %dynamic-update-slice.9), channel_id=3, replica_groups=mesh['grp'=8,'mem'=4] {'grp','mem'}, use_global_device_ids=true, to_apply=%add.1 | all-reduce | flops 2048 | bytes 16384
  633.3 39.7 %psum.53 = f32[64]{0:T(128)S(1)} all-reduce(f32[64]{0:T(128)S(1)} %get-tuple-element.481), channel_id=1, replica_groups=mesh['grp'=8,'mem'=4] {'grp','mem'}, use_global_device_ids=true, to_apply=%region_13.0 | all-reduce | flops 64 | bytes 512 | tf_op jit(solution)/shard_map/psum | solution.py:82
  675.9 3.0 scatter_custom_fusion.2
  678.9 3.6 fusion.363
  690.6 4.5 collective-permute-done.8
  695.1 5.3 collective-permute-done.9
  702.7 37.4 %all-reduce.12.cloned.1.call-done = f32[2048,64]{0,1:T(8,128)} async-done(((f32[2048,64]{0,1:T(8,128)}), f32[2048,64]{0,1:T(8,128)}) %all-reduce.12.cloned.1.call-update) | async-done | bytes 524304 | tf_op jit(solution)/shard_map/psum | solution.py:71
  812.4 10.7 %collective-permute-done.10 = f32[64,2048]{1,0:T(8,128)S(1)} collective-permute-done((f32[64,2048]{1,0:T(8,128)S(1)}, f32[64,2048]{1,0:T(8,128)S(1)}, u32[]{:S(2)}, u32[]{:S(2)}) %collective-permute-start.10) | collective-permute-done | bytes 524320 | tf_op jit(solution)/shard_map/ppermute | solution.py:23
  824.3 3.2 copy.39
  833.5 40.3 %all-reduce.2 = f32[2048]{0:T(1024)S(1)} all-reduce(f32[2048]{0:T(1024)S(1)} %dynamic-update-slice.10), channel_id=4, replica_groups=mesh['grp'=8,'mem'=4] {'grp','mem'}, use_global_device_ids=true, to_apply=%add.2 | all-reduce | flops 2048 | bytes 16384
  875.7 39.7 %psum.55 = f32[64]{0:T(128)S(1)} all-reduce(f32[64]{0:T(128)S(1)} %get-tuple-element.523), channel_id=1, replica_groups=mesh['grp'=8,'mem'=4] {'grp','mem'}, use_global_device_ids=true, to_apply=%region_19.0 | all-reduce | flops 64 | bytes 512 | tf_op jit(solution)/shard_map/psum | solution.py:82
  (678 shorter events, 327.4 us)
Async XLA Ops:
  7.2 1.2 copy-start
  7.2 245.8 %all-reduce.8.cloned.1.call-start = ((), (), s32[]{:S(2)}) async-start(), calls=%async_computation | async-start | bytes 1048576 | tf_op jit(solution)/shard_map/psum | solution.py:71
  19.5 16.1 %collective-permute-start = (f32[64,2048]{1,0:T(8,128)}, f32[64,2048]{1,0:T(8,128)}, u32[]{:S(2)}, u32[]{:S(2)}) collective-permute-start(f32[64,2048]{1,0:T(8,128)} %copy.29), channel_id=1, source_target_pairs={{4,0},{8,4},{12,8},{16,12},{20,16},{24,20},{28,24},{0,28},{5,1},{9... | collective-permute-start | bytes 1572872 | tf_op jit(solution)/shard_map/ppermute | solution.py:13
  24.0 12.4 %collective-permute-start.1 = (f32[64,2048]{1,0:T(8,128)}, f32[64,2048]{1,0:T(8,128)S(1)}, u32[]{:S(2)}, u32[]{:S(2)}) collective-permute-start(f32[64,2048]{1,0:T(8,128)} %copy.30), channel_id=1, source_target_pairs={{28,0},{0,4},{4,8},{8,12},{12,16},{16,20},{20,24},{24,28},{29,1},{... | collective-permute-start | bytes 1572872 | tf_op jit(solution)/shard_map/ppermute | solution.py:13
  38.4 456.5 %all-reduce.10.cloned.1.call-start = ((), (), s32[]{:S(2)}) async-start(), calls=%async_computation.1 | async-start | bytes 1048576 | tf_op jit(solution)/shard_map/psum | solution.py:71
  253.0 39.3 %copy-start.1 = (f32[2048,2048]{1,0:T(8,128)S(1)}, f32[2048,2048]{1,0:T(8,128)}, u32[]{:S(2)}) copy-start(f32[2048,2048]{1,0:T(8,128)} %get-tuple-element.572) | copy-start | bytes 50331652
  273.3 46.5 %copy-start.2 = (bf16[8,256,256]{2,1,0:T(8,128)(2,1)S(1)}, bf16[8,256,256]{2,1,0:T(8,128)(2,1)}, u32[]{:S(2)}) copy-start(bf16[8,256,256]{2,1,0:T(8,128)(2,1)} %param.14) | copy-start | bytes 3145732
  293.5 46.7 %copy-start.7 = (bf16[8,24,256]{2,1,0:T(8,128)(2,1)S(1)}, bf16[8,24,256]{2,1,0:T(8,128)(2,1)}, u32[]{:S(2)}) copy-start(bf16[8,24,256]{2,1,0:T(8,128)(2,1)} %param.15) | copy-start | bytes 294916
  317.1 14.6 %collective-permute-start.2 = (f32[64,2048]{1,0:T(8,128)}, f32[64,2048]{1,0:T(8,128)}, u32[]{:S(2)}, u32[]{:S(2)}) collective-permute-start(f32[64,2048]{1,0:T(8,128)} %bitcast.39), channel_id=1, source_target_pairs={{0,4},{4,8},{8,12},{12,16},{16,20},{20,24},{24,28},{28,0},{1,5},{5... | collective-permute-start | bytes 1572872 | tf_op jit(solution)/shard_map/ppermute | solution.py:23
  317.1 14.6 %collective-permute-start.3 = (f32[64,2048]{1,0:T(8,128)}, f32[64,2048]{1,0:T(8,128)}, u32[]{:S(2)}, u32[]{:S(2)}) collective-permute-start(f32[64,2048]{1,0:T(8,128)} %bitcast.39), channel_id=1, source_target_pairs={{4,0},{8,4},{12,8},{16,12},{20,16},{24,20},{28,24},{0,28},{5,1},{9... | collective-permute-start | bytes 1572872 | tf_op jit(solution)/shard_map/ppermute | solution.py:25
  385.4 0.8 copy-start.6
  429.1 0.8 copy-start.4
  439.6 10.4 %collective-permute-start.4 = (f32[64,2048]{1,0:T(8,128)}, f32[64,2048]{1,0:T(8,128)}, u32[]{:S(2)}, u32[]{:S(2)}) collective-permute-start(f32[64,2048]{1,0:T(8,128)} %copy.33), channel_id=1, source_target_pairs={{4,0},{8,4},{12,8},{16,12},{20,16},{24,20},{28,24},{0,28},{5,1},{9... | collective-permute-start | bytes 1572872 | tf_op jit(solution)/shard_map/ppermute | solution.py:13
  442.9 12.9 %collective-permute-start.5 = (f32[64,2048]{1,0:T(8,128)}, f32[64,2048]{1,0:T(8,128)}, u32[]{:S(2)}, u32[]{:S(2)}) collective-permute-start(f32[64,2048]{1,0:T(8,128)} %copy.34), channel_id=1, source_target_pairs={{28,0},{0,4},{4,8},{8,12},{12,16},{16,20},{20,24},{24,28},{29,1},{... | collective-permute-start | bytes 1572872 | tf_op jit(solution)/shard_map/ppermute | solution.py:13
  458.1 282.0 %all-reduce.12.cloned.1.call-start = ((), (), s32[]{:S(2)}) async-start(), calls=%async_computation.2 | async-start | bytes 1048576 | tf_op jit(solution)/shard_map/psum | solution.py:71
  564.8 13.4 %collective-permute-start.6 = (f32[64,2048]{1,0:T(8,128)S(1)}, f32[64,2048]{1,0:T(8,128)S(1)}, u32[]{:S(2)}, u32[]{:S(2)}) collective-permute-start(f32[64,2048]{1,0:T(8,128)S(1)} %bitcast.583), channel_id=1, source_target_pairs={{0,4},{4,8},{8,12},{12,16},{16,20},{20,24},{24,28},{28,0},{1,5},{5... | collective-permute-start | bytes 1572872 | tf_op jit(solution)/shard_map/ppermute | solution.py:23
  564.8 13.3 %collective-permute-start.7 = (f32[64,2048]{1,0:T(8,128)S(1)}, f32[64,2048]{1,0:T(8,128)S(1)}, u32[]{:S(2)}, u32[]{:S(2)}) collective-permute-start(f32[64,2048]{1,0:T(8,128)S(1)} %bitcast.584), channel_id=1, source_target_pairs={{4,0},{8,4},{12,8},{16,12},{20,16},{24,20},{28,24},{0,28},{5,1},{9... | collective-permute-start | bytes 1572872 | tf_op jit(solution)/shard_map/ppermute | solution.py:25
  631.2 0.8 copy-start.5
  674.3 0.8 copy-start.3
  684.9 10.2 %collective-permute-start.8 = (f32[64,2048]{1,0:T(8,128)}, f32[64,2048]{1,0:T(8,128)}, u32[]{:S(2)}, u32[]{:S(2)}) collective-permute-start(f32[64,2048]{1,0:T(8,128)} %copy.37), channel_id=1, source_target_pairs={{4,0},{8,4},{12,8},{16,12},{20,16},{24,20},{28,24},{0,28},{5,1},{9... | collective-permute-start | bytes 1572872 | tf_op jit(solution)/shard_map/ppermute | solution.py:13
  688.1 12.3 %collective-permute-start.9 = (f32[64,2048]{1,0:T(8,128)}, f32[64,2048]{1,0:T(8,128)}, u32[]{:S(2)}, u32[]{:S(2)}) collective-permute-start(f32[64,2048]{1,0:T(8,128)} %copy.38), channel_id=1, source_target_pairs={{28,0},{0,4},{4,8},{8,12},{12,16},{16,20},{20,24},{24,28},{29,1},{... | collective-permute-start | bytes 1572872 | tf_op jit(solution)/shard_map/ppermute | solution.py:13
  809.7 13.4 %collective-permute-start.10 = (f32[64,2048]{1,0:T(8,128)S(1)}, f32[64,2048]{1,0:T(8,128)S(1)}, u32[]{:S(2)}, u32[]{:S(2)}) collective-permute-start(f32[64,2048]{1,0:T(8,128)S(1)} %bitcast.580), channel_id=1, source_target_pairs={{0,4},{4,8},{8,12},{12,16},{16,20},{20,24},{24,28},{28,0},{1,5},{5... | collective-permute-start | bytes 1572872 | tf_op jit(solution)/shard_map/ppermute | solution.py:23
  809.7 13.3 %collective-permute-start.11 = (f32[64,2048]{1,0:T(8,128)S(1)}, f32[64,2048]{1,0:T(8,128)S(1)}, u32[]{:S(2)}, u32[]{:S(2)}) collective-permute-start(f32[64,2048]{1,0:T(8,128)S(1)} %bitcast.581), channel_id=1, source_target_pairs={{4,0},{8,4},{12,8},{16,12},{20,16},{24,20},{28,24},{0,28},{5,1},{9... | collective-permute-start | bytes 1572872 | tf_op jit(solution)/shard_map/ppermute | solution.py:25
  875.1 42.8 %copy-start.8 = (f32[8,64,256]{2,1,0:T(8,128)}, f32[8,64,256]{2,1,0:T(8,128)S(1)}, u32[]{:S(2)}) copy-start(f32[8,64,256]{2,1,0:T(8,128)S(1)} %multiply_subtract_fusion) | copy-start | bytes 1572868
Sparse Core Ops, SparseCore 0:
  38.5 39.3 all-reduce.7
  458.2 36.6 all-reduce.9
  702.8 37.2 all-reduce.11
